TPU v7x, 256 devices: a 8x8x2 block of a 8x8x16 slice. The times are simulated.
256 devices in a mesh: groups: 2 (over z), expert: 64 (over y, x), tensor: 2 (over core).
Axes of the slice: x: 8, y: 8, z: 2, core: 2. Of those that a mesh axis runs over, the one named last changes fastest.
The devices are a block of a 8x8x16 slice.
Arguments:
- tokens: bfloat16 [1024, 6144], P(('groups', 'expert')), parts along dimension 0, may hold values from -6 to 6
- routes: int32 [1024, 2], P(('groups', 'expert')), parts along dimension 0, may hold values from 0 to 3, all different within a row; in each aligned block of 8 rows (0 to 7, 8 to 15, ...) at most 5 rows name the same one
- router_logits: float32 [1024, 4], P(('groups', 'expert')), parts along dimension 0, may hold values from -9 to 310
- gate_weight: bfloat16 [64, 6144, 512], P('expert', None, 'tensor'), may hold values from -0.078125 to 0.078125
- up_weight: bfloat16 [64, 6144, 512], P('expert', None, 'tensor'), may hold values from -0.078125 to 0.078125
- down_weight: bfloat16 [64, 512, 6144], P('expert', 'tensor'), may hold values from -0.0625 to 0.0625
Outputs:
- layer_out: bfloat16 [1024, 6144], P(('groups', 'expert'), 'tensor'), parts along dimension 0
There are 2 independent parts, one for each index of `groups`. A program takes and returns all parts, laid end to end along the dimension named above; an argument that names none is the same for every part. Nothing has to cross between parts.
Inputs may be any that keep to these rules, and one draw needn't show every extreme that they name: `routes`: each row names two different experts. In the rows of one index of expert (aligned blocks of 8 rows) no expert is named more than 5 times, and in every draw some block names some expert exactly 5 times.
All inputs are finite; a program needn't handle non-finite values.
Results may differ from a plain program's by a relative error of at most 0.0049.
Values may be sent and summed in bfloat16 or wider, within the bound.
A program may use at most 64 MiB of HBM per device.

v0:
```python
import jax
import jax.numpy as jnp
from jax import lax
from jax.sharding import PartitionSpec as P

CAP = 5


def in_blocks(value, dim, devices):
    shape = value.shape
    blocks = value.reshape(*shape[:dim], devices, shape[dim] // devices, *shape[dim + 1 :])
    return jnp.moveaxis(blocks, dim, 0)


def sent_and_summed(value, axis, dim):
    blocks = in_blocks(value, dim, lax.axis_size(axis))
    arrived = lax.all_to_all(blocks, axis, split_axis=0, concat_axis=0, tiled=True)
    return arrived.sum(axis=0)


def piece_ends(length, count):
    lap = length // count
    if lap >= 8:
        lap -= lap % 8
    return [lap * k for k in range(1, count)]


def joined_along(blocks, dim):
    blocks = jnp.moveaxis(blocks, 0, dim)
    shape = blocks.shape
    return blocks.reshape(*shape[:dim], shape[dim] * shape[dim + 1], *shape[dim + 2 :])


def exchange_in_pieces(value, axis, pieces, split_dim, concat_dim):
    blocks = in_blocks(value, split_dim, lax.axis_size(axis))
    widest = max(range(1, max(2, blocks.ndim - 1)), key=lambda d: blocks.shape[d])
    finished = []
    for share in jnp.split(blocks, piece_ends(blocks.shape[widest], pieces), axis=widest):
        if share.size:
            finished.append(lax.all_to_all(share, axis, split_axis=0, concat_axis=0, tiled=True))
    return joined_along(jnp.concatenate(finished, axis=widest), concat_dim)


def shards(tokens, routes, router_logits, gate_weight, up_weight, down_weight):
    local_tokens = tokens.shape[0]
    width = tokens.shape[1]
    experts = router_logits.shape[1]
    devices = lax.axis_size("expert")
    segments = devices // experts
    capacity = CAP
    expert_ids = jnp.arange(experts, dtype=jnp.int32)
    picked = jnp.take_along_axis(router_logits, routes, axis=1)
    route_weight = jax.nn.softmax(picked, axis=1)
    onehot = (routes[:, :, None] == expert_ids[None, None, :]).astype(jnp.int32)
    flat_hot = onehot.reshape(local_tokens * 2, experts)
    earlier = jnp.cumsum(flat_hot, axis=0) - flat_hot
    slot_index = jnp.sum(earlier * flat_hot, axis=1).reshape(local_tokens, 2)
    target = routes * capacity + slot_index
    cell_ids = jnp.arange(experts * capacity, dtype=jnp.int32)
    placed = target[:, :, None] == cell_ids[None, None, :]
    pick_matrix = jnp.any(placed, axis=1).astype(jnp.bfloat16)
    mix_matrix = jnp.sum(route_weight[:, :, None] * placed.astype(jnp.float32), axis=1)
    buffer = jnp.einsum(
        "tc,td->cd", pick_matrix, tokens, preferred_element_type=jnp.float32
    ).astype(jnp.bfloat16)
    buffer = buffer.reshape(experts, capacity, width)
    gate_local = gate_weight[0]
    up_local = up_weight[0]
    down_local = down_weight[0]
    outgoing = jnp.repeat(buffer, segments, axis=0)
    half_width = width // lax.axis_size("tensor")
    own_columns = lax.dynamic_slice_in_dim(
        outgoing, lax.axis_index("tensor") * half_width, half_width, 2
    )
    slot_rows = lax.all_gather(
        lax.all_to_all(own_columns, "expert", split_axis=0, concat_axis=0, tiled=True),
        "tensor",
        axis=2,
        tiled=True,
    )
    sources = slot_rows.shape[0]
    items = slot_rows.shape[1]
    flattened = slot_rows.reshape(sources * items, slot_rows.shape[2])
    gate_out = jnp.dot(flattened, gate_local, preferred_element_type=jnp.float32)
    up_out = jnp.dot(flattened, up_local, preferred_element_type=jnp.float32)
    hidden = (jax.nn.silu(gate_out) * up_out).astype(jnp.bfloat16)
    result = jnp.dot(hidden, down_local, preferred_element_type=jnp.float32)
    partial_out = result.reshape(sources, items, width)
    reduced = sent_and_summed(partial_out, "tensor", 2)
    returned = exchange_in_pieces(reduced, "expert", 2, 0, 0)
    columns_here = returned.shape[2]
    gathered_out = jnp.sum(returned.reshape(experts, segments, capacity, columns_here), axis=1)
    gathered_out = gathered_out.reshape(experts * capacity, columns_here)
    layer_out = jnp.dot(
        mix_matrix,
        gathered_out,
        precision=lax.Precision.HIGHEST,
        preferred_element_type=jnp.float32,
    )
    return layer_out.astype(jnp.bfloat16)


def solution(mesh):
    return jax.shard_map(
        shards,
        mesh=mesh,
        in_specs=(
            P(("groups", "expert"), None),
            P(("groups", "expert"), None),
            P(("groups", "expert"), None),
            P("expert", None, "tensor"),
            P("expert", None, "tensor"),
            P("expert", "tensor", None),
        ),
        out_specs=P(("groups", "expert"), "tensor"),
        check_vma=False,
    )
```

profile of v0, /device:TPU:514, one launch (start us, length us, event | category | flops | bytes accessed | tf_op | source)
XLA Modules:
  0.0 314.4 jit_solution(12775214072166252372)
XLA Ops:
  6.6 0.9 copy.70
  8.1 1.9 convolution_convert_fusion
  10.0 1.1 reshape.56
  11.1 0.8 broadcast_in_dim.2
  12.1 94.5 %all_to_all.20 = bf16[64,5,3072]{2,1,0:T(8,128)(2,1)} all-to-all(bf16[64,5,3072]{2,1,0:T(8,128)(2,1)S(1)} %constant_dynamic-slice_fusion), channel_id=1, replica_groups=mesh['groups'=2,'expert'=64,'tensor'=2] {'expert'}, dimensions={0} | all-to-all | bytes 3932160 | tf_op jit(solution)/shard_map/all_to_all | solution.py:76
  106.7 4.7 %copy.91 = bf16[6144,256]{1,0:T(8,128)(2,1)} copy(bf16[6144,256]{0,1:T(8,128)(2,1)} %bitcast.38) | data formatting | bytes 6291456 | tf_op jit(solution)/shard_map/dot_general | solution.py:87
  111.4 27.0 %all-gather.2.cloned.1.call-done = bf16[64,5,6144]{2,1,0:T(8,128)(2,1)} async-done(((bf16[64,5,3072]{2,1,0:T(8,128)(2,1)}), bf16[64,5,6144]{2,1,0:T(8,128)(2,1)}) %all-gather.2.cloned.1.call-update) | async-done | bytes 3932176 | tf_op jit(solution)/shard_map/all_gather | solution.py:75
  138.4 7.7 %reshape.58 = bf16[320,6144]{1,0:T(8,128)(2,1)} reshape(bf16[64,5,6144]{2,1,0:T(8,128)(2,1)} %all-gather.2.cloned.1.call-done) | data formatting | bytes 7864320 | tf_op jit(solution)/shard_map/reshape | solution.py:83
  146.1 3.4 %fusion.2 = f32[320,256]{1,0:T(8,128)S(1)} fusion(bf16[320,6144]{1,0:T(8,128)(2,1)} %reshape.58, bf16[1,6144,256]{2,1,0:T(8,128)(2,1)S(1)} %copy-done), kind=kOutput, calls=%fused_computation.7 | convolution fusion | flops 1006632960 | bytes 7405568 | tf_op jit(solution)/shard_map/dot_general | solution.py:84
  149.6 0.8 copy-done.6
  150.4 1.8 fusion.7
  152.2 1.0 dot_general.24
  153.2 1.2 convolution_bitcast_fusion
  154.5 0.9 copy.81
  155.4 11.3 %all_to_all.21 = f32[2,64,5,3072]{3,1,2,0:T(8,128)} all-to-all(f32[2,64,5,3072]{3,1,2,0:T(8,128)S(1)} %copy.81), channel_id=1, replica_groups=mesh['groups'=2,'expert'=64,'tensor'=2] {'tensor'}, dimensions={0} | all-to-all | bytes 15728640 | tf_op jit(solution)/shard_map/all_to_all | solution.py:17
  166.8 6.3 %reduce_sum.48 = f32[64,5,3072]{2,0,1:T(8,128)} reduce(f32[2,64,5,3072]{3,1,2,0:T(8,128)} %all_to_all.21, f32[]{:T(128)} %constant.36.clone.1), dimensions={0}, to_apply=%region_6.7 | reduce | flops 983040 | bytes 11796484 | tf_op jit(solution)/shard_map/reduce_sum | solution.py:18
  173.0 1.5 split.8
  174.6 2.4 copy.83
  177.0 13.7 %all-to-all-start.2 = ((f32[64,1,2,3072]{3,2,1,0:T(2,128)}), f32[64,1,2,3072]{3,2,1,0:T(2,128)}, u32[]{:S(2)}, u32[]{:S(2)}) async-start(f32[64,1,2,3072]{3,2,1,0:T(2,128)} %copy.83), calls=%async_computation.2 | async-start | bytes 3145728 | tf_op jit(solution)/shard_map/all_to_all | solution.py:40
  190.7 1.9 split.9
  192.6 3.8 %copy.84 = f32[64,1,3,3072]{3,1,2,0:T(1,128)} copy(f32[64,1,3,3072]{3,0,2,1:T(8,128)S(1)} %split.9) | data formatting | bytes 4718592 | tf_op jit(solution)/shard_map/split | solution.py:38
  196.4 35.4 %all-to-all-done.2 = f32[64,1,2,3072]{3,2,1,0:T(2,128)} async-done(((f32[64,1,2,3072]{3,2,1,0:T(2,128)}), f32[64,1,2,3072]{3,2,1,0:T(2,128)}, u32[]{:S(2)}, u32[]{:S(2)}) %all-to-all-start.2) | async-done | bytes 1572896 | tf_op jit(solution)/shard_map/all_to_all | solution.py:40
  231.8 8.6 %all-to-all-start.3 = ((f32[64,1,3,3072]{3,1,2,0:T(1,128)}), f32[64,1,3,3072]{3,1,2,0:T(1,128)S(1)}, u32[]{:S(2)}, u32[]{:S(2)}) async-start(f32[64,1,3,3072]{3,1,2,0:T(1,128)} %copy.84), calls=%async_computation.3 | async-start | bytes 4718592 | tf_op jit(solution)/shard_map/all_to_all | solution.py:40
  240.6 0.7 gather_fusion
  242.0 3.1 copy.85
  245.0 51.5 %all-to-all-done.3 = f32[64,1,3,3072]{3,1,2,0:T(1,128)S(1)} async-done(((f32[64,1,3,3072]{3,1,2,0:T(1,128)}), f32[64,1,3,3072]{3,1,2,0:T(1,128)S(1)}, u32[]{:S(2)}, u32[]{:S(2)}) %all-to-all-start.3) | async-done | bytes 2359328 | tf_op jit(solution)/shard_map/all_to_all | solution.py:40
  296.9 1.0 copy-done.4
  297.9 2.3 pad_maximum_fusion
  300.3 3.6 %reduce_sum.49 = f32[4,5,3072]{2,0,1:T(4,128)} reduce(f32[4,16,5,3072]{3,1,0,2:T(8,128)} %bitcast.35, f32[]{:T(128)} %constant.36.clone.1), dimensions={1}, to_apply=%region_7.8 | reduce | flops 921600 | bytes 4177924 | tf_op jit(solution)/shard_map/reduce_sum | solution.py:92
  303.9 1.1 copy.87
  305.0 0.8 reshape.60
  305.7 1.9 convolution_convert_fusion.1
  (34 shorter events, 2.3 us)
Async XLA Ops:
  6.5 139.6 %copy-start = (bf16[1,6144,256]{2,1,0:T(8,128)(2,1)S(1)}, bf16[1,6144,256]{2,1,0:T(8,128)(2,1)}, u32[]{:S(2)}) copy-start(bf16[1,6144,256]{2,1,0:T(8,128)(2,1)} %param.9) | copy-start | bytes 9437188
  6.6 131.9 %all-gather.2.cloned.1.call-start = ((), (), s32[]{:S(2)}) async-start(), calls=%async_computation.4 | async-start | bytes 9437184 | tf_op jit(solution)/shard_map/all_gather | solution.py:75
  146.1 3.5 %copy-start.5 = (bf16[320,6144]{1,0:T(8,128)(2,1)S(1)}, bf16[320,6144]{1,0:T(8,128)(2,1)}, u32[]{:S(2)}) copy-start(bf16[320,6144]{1,0:T(8,128)(2,1)} %reshape.58) | copy-start | bytes 11796484
  146.1 4.3 %copy-start.6 = (bf16[1,6144,256]{2,1,0:T(8,128)(2,1)S(1)}, bf16[1,6144,256]{2,1,0:T(8,128)(2,1)}, u32[]{:S(2)}) copy-start(bf16[1,6144,256]{2,1,0:T(8,128)(2,1)} %param.10) | copy-start | bytes 9437188
  150.4 2.8 copy-start.3
  177.0 54.8 %all-to-all-start.2 = ((f32[64,1,2,3072]{3,2,1,0:T(2,128)}), f32[64,1,2,3072]{3,2,1,0:T(2,128)}, u32[]{:S(2)}, u32[]{:S(2)}) async-start(f32[64,1,2,3072]{3,2,1,0:T(2,128)} %copy.83), calls=%async_computation.2 | async-start | bytes 3145728 | tf_op jit(solution)/shard_map/all_to_all | solution.py:40
  196.4 44.2 %copy-start.2 = (f32[8,4]{0,1:T(4,128)S(1)}, f32[8,4]{0,1:T(4,128)}, u32[]{:S(2)}) copy-start(f32[8,4]{0,1:T(4,128)} %param.8) | copy-start | bytes 388
  231.8 64.7 %all-to-all-start.3 = ((f32[64,1,3,3072]{3,1,2,0:T(1,128)}), f32[64,1,3,3072]{3,1,2,0:T(1,128)S(1)}, u32[]{:S(2)}, u32[]{:S(2)}) async-start(f32[64,1,3,3072]{3,1,2,0:T(1,128)} %copy.84), calls=%async_computation.3 | async-start | bytes 4718592 | tf_op jit(solution)/shard_map/all_to_all | solution.py:40
  296.5 1.4 copy-start.4
  297.9 9.6 %copy-start.1 = (bf16[1,6144,256]{2,1,0:T(8,128)(2,1)S(1)}, bf16[1,6144,256]{2,1,0:T(8,128)(2,1)}, u32[]{:S(2)}) copy-start(bf16[1,6144,256]{2,1,0:T(8,128)(2,1)} %param.9) | copy-start | bytes 9437188
Sparse Core Ops, SparseCore 0:
  106.8 31.5 all-gather.1
where the time goes:
time: 315 us; the launch traced here: 314 us
  waiting for transfers between devices  114 us (36%)
  blocking collectives  106 us (34%)
  local copies, waits for them, and re-layouts  35.5 us (11%)
  starting transfers between devices  22.3 us (7%)
  between operations  13.6 us (4%)
  other arithmetic  13.1 us (4%)
  matrix products  10.2 us (3%)
    all_to_all x1, blocking collectives, shards(): lax.all_to_all(own_columns, 'expert', split_axis=0, concat_axis=0, tiled=...  94.5 us
    all_to_all x2, waiting for transfers between devices, exchange_in_pieces(): lax.all_to_all(share, axis, split_axis=0, concat_axis=0, tiled=True)  86.8 us
    all_gather x1, waiting for transfers between devices, shards(): lax.all_gather(lax.all_to_all(own_columns, 'expert', split_axis=0, concat...  27 us
    all_to_all x2, starting transfers between devices, exchange_in_pieces(): lax.all_to_all(share, axis, split_axis=0, concat_axis=0, tiled=True)  22.3 us
    all_to_all x1, blocking collectives, sent_and_summed(): lax.all_to_all(blocks, axis, split_axis=0, concat_axis=0, tiled=True)  11.3 us
    split x4, local copies, waits for them, and re-layouts, exchange_in_pieces(): jnp.split(blocks, piece_ends(blocks.shape[widest], pieces), axis=widest)  9.65 us
    reshape x1, local copies, waits for them, and re-layouts, shards(): flattened = slot_rows.reshape(sources * items, slot_rows.shape[2])  7.69 us
  transfers between devices with their start and end apart: 3, of which 3 were waited for; matrix products, arithmetic and copies ran while one was open for 5% of the time, Pallas kernels for 0%

commit v1 on v0

--- a/solution.py
+++ b/solution.py
@@ -72,11 +72,17 @@
     own_columns = lax.dynamic_slice_in_dim(
         outgoing, lax.axis_index("tensor") * half_width, half_width, 2
     )
-    slot_rows = lax.all_gather(
-        lax.all_to_all(own_columns, "expert", split_axis=0, concat_axis=0, tiled=True),
-        "tensor",
+    slot_rows = jnp.concatenate(
+        jax.lax.all_to_all(
+            jnp.stack(
+                jax.lax.axis_size("tensor")
+                * [lax.all_to_all(own_columns, "expert", split_axis=0, concat_axis=0, tiled=True)]
+            ),
+            "tensor",
+            0,
+            0,
+        ),
         axis=2,
-        tiled=True,
     )
     sources = slot_rows.shape[0]
     items = slot_rows.shape[1]

time: 315 us -> 301 us (0.956)
  the two profiles are of different devices: /device:TPU:514 before, /device:TPU:640 now
where the time goes in v1:
time: 301 us; the launch traced here: 300 us
  waiting for transfers between devices  157 us (52%)
  starting transfers between devices  62 us (21%)
  local copies, waits for them, and re-layouts  41.5 us (14%)
  blocking collectives  18.3 us (6%)
  other arithmetic  13.4 us (4%)
  matrix products  8.05 us (3%)
    all_to_all x2, waiting for transfers between devices, exchange_in_pieces(): lax.all_to_all(share, axis, split_axis=0, concat_axis=0, tiled=True)  85.8 us
    all_to_all x1, waiting for transfers between devices, shards(): lax.all_to_all(own_columns, 'expert', split_axis=0, concat_axis=0, tiled=...  71.2 us
    all_to_all x2, starting transfers between devices, exchange_in_pieces(): lax.all_to_all(share, axis, split_axis=0, concat_axis=0, tiled=True)  40.7 us
    all_to_all x1, starting transfers between devices, shards(): lax.all_to_all(own_columns, 'expert', split_axis=0, concat_axis=0, tiled=...  21.3 us
    all_to_all x1, blocking collectives, sent_and_summed(): lax.all_to_all(blocks, axis, split_axis=0, concat_axis=0, tiled=True)  11.3 us
    split x4, local copies, waits for them, and re-layouts, exchange_in_pieces(): jnp.split(blocks, piece_ends(blocks.shape[widest], pieces), axis=widest)  9.65 us
    all_to_all x1, blocking collectives, shards(): jax.lax.all_to_all(jnp.stack(jax.lax.axis_size('tensor') * [lax.all_to_al...  6.91 us
    reduce_sum x1, other arithmetic, sent_and_summed(): return arrived.sum(axis=0)  6.28 us
  transfers between devices with their start and end apart: 3, of which 3 were waited for; matrix products, arithmetic and copies ran while one was open for 5% of the time, Pallas kernels for 0%

profile of v1, /device:TPU:640, one launch (start us, length us, event | category | flops | bytes accessed | tf_op | source)
XLA Modules:
  0.0 300.3 jit_solution(3893910572671750895)
XLA Ops:
  0.0 0.9 copy.87
  1.5 1.9 convolution_convert_fusion
  3.4 1.1 reshape.56
  5.3 2.0 constant_dynamic-slice_fusion
  7.3 21.3 %all-to-all-start = ((bf16[64,5,3072]{2,1,0:T(8,128)(2,1)}), bf16[64,5,3072]{2,1,0:T(8,128)(2,1)}, u32[]{:S(2)}, u32[]{:S(2)}) async-start(bf16[64,5,3072]{2,1,0:T(8,128)(2,1)} %constant_dynamic-slice_fusion), calls=%async_computation | async-start | bytes 6291456 | tf_op jit(solution)/shard_map/all_to_all | solution.py:79
  28.6 4.6 %copy.110 = bf16[6144,256]{1,0:T(8,128)(2,1)} copy(bf16[6144,256]{0,1:T(8,128)(2,1)} %bitcast.50) | data formatting | bytes 6291456 | tf_op jit(solution)/shard_map/dot_general | solution.py:93
  33.2 71.2 %all-to-all-done = bf16[64,5,3072]{2,1,0:T(8,128)(2,1)} async-done(((bf16[64,5,3072]{2,1,0:T(8,128)(2,1)}), bf16[64,5,3072]{2,1,0:T(8,128)(2,1)}, u32[]{:S(2)}, u32[]{:S(2)}) %all-to-all-start) | async-done | bytes 1966112 | tf_op jit(solution)/shard_map/all_to_all | solution.py:79
  104.4 3.2 %copy.116 = bf16[64,5,3072]{2,0,1:T(8,128)(2,1)S(1)} copy(bf16[64,5,3072]{2,1,0:T(8,128)(2,1)} %all-to-all-done) | data formatting | bytes 3932160 | tf_op jit(solution)/shard_map/all_to_all | solution.py:79
  107.9 6.9 %all_to_all.25 = bf16[2,64,5,3072]{3,1,2,0:T(8,128)(2,1)S(1)} all-to-all(bf16[2,64,5,3072]{3,1,2,0:T(8,128)(2,1)S(1)} %pad_maximum_fusion), channel_id=1, replica_groups=mesh['groups'=2,'expert'=64,'tensor'=2] {'tensor'}, dimensions={0} | all-to-all | bytes 7864320 | tf_op jit(solution)/shard_map/all_to_all | solution.py:76
  114.8 5.9 %copy.97 = bf16[64,5,2,3072]{3,2,1,0:T(2,128)(2,1)} copy(bf16[64,5,2,3072]{3,0,1,2:T(8,128)(2,1)S(1)} %bitcast.43) | data formatting | bytes 7864320 | tf_op jit(solution)/shard_map/reshape | solution.py:75
  120.7 3.1 %copy.112 = bf16[40,8,2,3072]{3,1,2,0:T(8,128)(2,1)S(1)} copy(bf16[40,8,2,3072]{3,2,1,0:T(2,128)(2,1)} %bitcast.44) | data formatting | bytes 7864320
  123.9 1.2 fusion.2
  125.8 1.8 fusion.7
  127.6 1.0 dot_general.24
  128.6 1.2 convolution_bitcast_fusion
  129.8 0.9 copy.100
  130.8 11.3 %all_to_all.26 = f32[2,64,5,3072]{3,1,2,0:T(8,128)} all-to-all(f32[2,64,5,3072]{3,1,2,0:T(8,128)S(1)} %copy.100), channel_id=1, replica_groups=mesh['groups'=2,'expert'=64,'tensor'=2] {'tensor'}, dimensions={0} | all-to-all | bytes 15728640 | tf_op jit(solution)/shard_map/all_to_all | solution.py:17
  142.1 6.3 %reduce_sum.48 = f32[64,5,3072]{2,0,1:T(8,128)} reduce(f32[2,64,5,3072]{3,1,2,0:T(8,128)} %all_to_all.26, f32[]{:T(128)} %constant.36.clone.1), dimensions={0}, to_apply=%region_6.7 | reduce | flops 983040 | bytes 11796484 | tf_op jit(solution)/shard_map/reduce_sum | solution.py:18
  148.4 1.5 split.8
  150.0 2.4 copy.102
  152.4 31.4 %all-to-all-start.3 = ((f32[64,1,2,3072]{3,2,1,0:T(2,128)}), f32[64,1,2,3072]{3,2,1,0:T(2,128)}, u32[]{:S(2)}, u32[]{:S(2)}) async-start(f32[64,1,2,3072]{3,2,1,0:T(2,128)} %copy.102), calls=%async_computation.3 | async-start | bytes 3145728 | tf_op jit(solution)/shard_map/all_to_all | solution.py:40
  183.8 1.9 split.9
  185.7 3.8 %copy.103 = f32[64,1,3,3072]{3,1,2,0:T(1,128)} copy(f32[64,1,3,3072]{3,0,2,1:T(8,128)S(1)} %split.9) | data formatting | bytes 4718592 | tf_op jit(solution)/shard_map/split | solution.py:38
  189.5 34.6 %all-to-all-done.3 = f32[64,1,2,3072]{3,2,1,0:T(2,128)} async-done(((f32[64,1,2,3072]{3,2,1,0:T(2,128)}), f32[64,1,2,3072]{3,2,1,0:T(2,128)}, u32[]{:S(2)}, u32[]{:S(2)}) %all-to-all-start.3) | async-done | bytes 1572896 | tf_op jit(solution)/shard_map/all_to_all | solution.py:40
  224.1 9.3 %all-to-all-start.4 = ((f32[64,1,3,3072]{3,1,2,0:T(1,128)}), f32[64,1,3,3072]{3,1,2,0:T(1,128)S(1)}, u32[]{:S(2)}, u32[]{:S(2)}) async-start(f32[64,1,3,3072]{3,1,2,0:T(1,128)} %copy.103), calls=%async_computation.4 | async-start | bytes 4718592 | tf_op jit(solution)/shard_map/all_to_all | solution.py:40
  235.0 3.1 %copy.104 = f32[64,1,2,3072]{3,0,2,1:T(8,128)} copy(f32[64,1,2,3072]{3,2,1,0:T(2,128)} %all-to-all-done.3) | data formatting | bytes 3145728 | tf_op jit(solution)/shard_map/all_to_all | solution.py:40
  238.1 51.2 %all-to-all-done.4 = f32[64,1,3,3072]{3,1,2,0:T(1,128)S(1)} async-done(((f32[64,1,3,3072]{3,1,2,0:T(1,128)}), f32[64,1,3,3072]{3,1,2,0:T(1,128)S(1)}, u32[]{:S(2)}, u32[]{:S(2)}) %all-to-all-start.4) | async-done | bytes 2359328 | tf_op jit(solution)/shard_map/all_to_all | solution.py:40
  289.7 1.0 copy-done.4
  290.7 2.3 pad_maximum_fusion.1
  293.0 3.6 %reduce_sum.49 = f32[4,5,3072]{2,0,1:T(4,128)} reduce(f32[4,16,5,3072]{3,1,0,2:T(8,128)} %bitcast.42, f32[]{:T(128)} %constant.36.clone.1), dimensions={1}, to_apply=%region_7.8 | reduce | flops 921600 | bytes 4177924 | tf_op jit(solution)/shard_map/reduce_sum | solution.py:98
  296.6 1.1 copy.106
  298.5 1.9 convolution_convert_fusion.1
  (34 shorter events, 5.1 us)
Async XLA Ops:
  0.0 123.9 %copy-start = (bf16[1,6144,256]{2,1,0:T(8,128)(2,1)S(1)}, bf16[1,6144,256]{2,1,0:T(8,128)(2,1)}, u32[]{:S(2)}) copy-start(bf16[1,6144,256]{2,1,0:T(8,128)(2,1)} %param.9) | copy-start | bytes 9437188
  7.3 97.1 %all-to-all-start = ((bf16[64,5,3072]{2,1,0:T(8,128)(2,1)}), bf16[64,5,3072]{2,1,0:T(8,128)(2,1)}, u32[]{:S(2)}, u32[]{:S(2)}) async-start(bf16[64,5,3072]{2,1,0:T(8,128)(2,1)} %constant_dynamic-slice_fusion), calls=%async_computation | async-start | bytes 6291456 | tf_op jit(solution)/shard_map/all_to_all | solution.py:79
  123.9 1.9 copy-start.5
  125.8 2.8 copy-start.3
  152.4 71.8 %all-to-all-start.3 = ((f32[64,1,2,3072]{3,2,1,0:T(2,128)}), f32[64,1,2,3072]{3,2,1,0:T(2,128)}, u32[]{:S(2)}, u32[]{:S(2)}) async-start(f32[64,1,2,3072]{3,2,1,0:T(2,128)} %copy.102), calls=%async_computation.3 | async-start | bytes 3145728 | tf_op jit(solution)/shard_map/all_to_all | solution.py:40
  189.5 44.2 %copy-start.2 = (f32[8,4]{0,1:T(4,128)S(1)}, f32[8,4]{0,1:T(4,128)}, u32[]{:S(2)}) copy-start(f32[8,4]{0,1:T(4,128)} %param.8) | copy-start | bytes 388
  224.1 65.1 %all-to-all-start.4 = ((f32[64,1,3,3072]{3,1,2,0:T(1,128)}), f32[64,1,3,3072]{3,1,2,0:T(1,128)S(1)}, u32[]{:S(2)}, u32[]{:S(2)}) async-start(f32[64,1,3,3072]{3,1,2,0:T(1,128)} %copy.103), calls=%async_computation.4 | async-start | bytes 4718592 | tf_op jit(solution)/shard_map/all_to_all | solution.py:40
  289.3 1.4 copy-start.4
  290.7 9.6 %copy-start.1 = (bf16[1,6144,256]{2,1,0:T(8,128)(2,1)S(1)}, bf16[1,6144,256]{2,1,0:T(8,128)(2,1)}, u32[]{:S(2)}) copy-start(bf16[1,6144,256]{2,1,0:T(8,128)(2,1)} %param.9) | copy-start | bytes 9437188
